TPU v7x, 256 devices: a 8x8x2 block of a 8x8x16 slice. The times are simulated.
256 devices in a mesh: groups: 2 (over z), tensor: 128 (over x, y, core).
Axes of the slice: x: 8, y: 8, z: 2, core: 2. Of those that a mesh axis runs over, the one named last changes fastest.
The devices are a block of a 8x8x16 slice.
Arguments:
- image_features: bfloat16 [256, 12800], P('groups', 'tensor'), parts along dimension 0, may hold values from -6 to 6
- image_counts: int32 [4], P('groups'), parts along dimension 0, may hold values from 1 to 64, 80 in all
- slot_position: int32 [256], P('groups'), parts along dimension 0, may hold values from 0 to 255, as said below
- text_ids: int32 [512], P('groups'), parts along dimension 0, may hold values from 0 to 49151
- norm_gain: float32 [12800], replicated, may hold values from 0.5 to 1.5
- norm_bias: float32 [12800], replicated, may hold values from -3 to 3
- proj_first: bfloat16 [6144, 12800], P('tensor'), may hold values from -0.0546875 to 0.0546875
- proj_second: bfloat16 [6144, 6144], P('tensor'), may hold values from -0.078125 to 0.078125
- embedding: bfloat16 [6144, 49152], P('tensor'), may hold values from -6 to 6
- rms_gain: float32 [6144], replicated, may hold values from 0.5 to 1.5
- gate_weight: bfloat16 [6144, 16384], P(None, 'tensor'), may hold values from -0.3125 to 0.3125
- up_weight: bfloat16 [6144, 16384], P(None, 'tensor'), may hold values from -0.3125 to 0.3125
- down_weight: bfloat16 [16384, 6144], P('tensor'), may hold values from -0.046875 to 0.046875
- output_grad: bfloat16 [512, 6144], P('groups', 'tensor'), parts along dimension 0, may hold values from -6 to 6
Outputs:
- input_grad: float32 [512, 6144], P('groups', 'tensor'), parts along dimension 0
- second_grad: float32 [12288, 6144], P(('groups', 'tensor')), parts along dimension 0
There are 2 independent parts, one for each index of `groups`. A program takes and returns all parts, laid end to end along the dimension named above; an argument that names none is the same for every part. Nothing has to cross between parts.
Inputs may be any that keep to these rules, and one draw needn't show every extreme that they name: `image_counts`: the counts sum to 80. `slot_position`: the 128 positions are distinct.
All inputs are finite; a program needn't handle non-finite values.
Results may differ from a plain program's by a relative error of at most 0.0079.
Values may be sent and summed in bfloat16 or wider, within the bound.
A program may use at most 128 MiB of HBM per device.

v0:
```python
import jax
import jax.numpy as jnp
from jax import lax
from jax.sharding import Mesh
from jax.sharding import PartitionSpec as P

LIVE = 80
TENSOR = ("tensor_0", "tensor_1", "tensor_2")
GROUPS_TENSOR = ("groups", "tensor_0", "tensor_1", "tensor_2")


def in_order(parts, dim):
    shape = list(parts.shape[1:])
    shape[dim] *= parts.shape[0]
    return jnp.moveaxis(parts, 0, dim).reshape(shape)


def all_blocks(x, axes, order):
    parts = x
    for k in order:
        parts = lax.all_gather(parts, axes[k])
    done = order[::-1]
    back = [done.index(k) for k in range(len(axes))]
    parts = parts.transpose(*back, *range(len(axes), parts.ndim))
    return parts.reshape(-1, *x.shape)


def whole_of(x, axes, order, dim):
    return in_order(all_blocks(x, axes, order), dim)


def own_block(parts, axes, order):
    inside = parts.shape[1:]
    parts = parts.reshape(*(lax.axis_size(a) for a in axes), *inside)
    parts = jnp.moveaxis(parts, order, range(len(axes))).reshape(-1, *inside)
    for k in order:
        parts = lax.psum_scatter(parts, axes[k], scatter_dimension=0, tiled=True)
    return parts[0]


def in_blocks(x, dim, size):
    before, after = (x.shape[:dim], x.shape[dim + 1 :])
    return jnp.moveaxis(x.reshape(*before, size, -1, *after), dim, 0)


def scatter_axes(x, axes, order, dim):
    size = lax.axis_size(axes)
    return own_block(in_blocks(x, dim, size), axes, order)


def one_axis_at_a_time(x, axes):
    for axis in axes:
        x = lax.psum(x, axis)
    return x


def layer_norm(rows_in, gain_in, bias_in):
    values = rows_in.astype(jnp.float32)
    centre = values - jnp.mean(values, axis=-1, keepdims=True)
    spread = jnp.mean(centre * centre, axis=-1, keepdims=True)
    return (centre * lax.rsqrt(spread + 1e-05) * gain_in + bias_in).astype(jnp.bfloat16)


def on_device(
    image_features,
    image_counts,
    slot_position,
    text_ids,
    norm_gain,
    norm_bias,
    proj_first,
    proj_second,
    embedding,
    rms_gain,
    gate_weight,
    up_weight,
    down_weight,
    output_grad,
):
    slot_total = image_features.shape[0]
    per_image = slot_total // image_counts.shape[0]
    seq_len = output_grad.shape[0]
    model_width = gate_weight.shape[0]
    col_count = output_grad.shape[1]
    slot_ids = jnp.arange(slot_total, dtype=jnp.int32)
    is_live = slot_ids % per_image < jnp.repeat(
        image_counts, per_image, total_repeat_length=slot_total
    )
    packed_order = jnp.argsort(jnp.where(is_live, 0, 1).astype(jnp.int32), stable=True)[:LIVE]
    gathered = whole_of(image_features[packed_order], TENSOR, (0, 1, 2), 1)
    positions = slot_position[packed_order]
    in_use = jnp.ones((LIVE,), dtype=bool)
    normed = layer_norm(gathered, norm_gain, norm_bias)
    hidden_pre = lax.dot_general(
        normed, proj_first, (((1,), (1,)), ((), ())), preferred_element_type=jnp.float32
    )
    act_cols = jax.nn.gelu(hidden_pre, approximate=False).astype(jnp.bfloat16)
    act_full = lax.all_gather(act_cols, TENSOR, axis=1, tiled=True)
    projected = lax.dot_general(
        act_full, proj_second, (((1,), (1,)), ((), ())), preferred_element_type=jnp.float32
    ).astype(jnp.bfloat16)
    target = jnp.where(in_use, positions, seq_len)
    text_rows = jnp.take(embedding, text_ids, axis=1).T
    tokens = text_rows.at[target].set(projected, mode="drop")
    full_tokens = lax.all_gather(tokens, TENSOR, axis=1, tiled=True)
    values = full_tokens.astype(jnp.float32)
    inverse = lax.rsqrt(jnp.mean(values * values, axis=-1, keepdims=True) + 1e-05)
    normed_tokens = (values * inverse * rms_gain).astype(jnp.bfloat16)
    gate_out = jnp.dot(normed_tokens, gate_weight, preferred_element_type=jnp.float32)
    up_out = jnp.dot(normed_tokens, up_weight, preferred_element_type=jnp.float32)
    hidden_grad = lax.dot_general(
        lax.all_gather(output_grad, TENSOR, axis=1, tiled=True),
        down_weight,
        (((1,), (1,)), ((), ())),
        preferred_element_type=jnp.float32,
    )
    sig_gate = jax.nn.sigmoid(gate_out)
    gate_grad = (hidden_grad * up_out * sig_gate * (1.0 + gate_out * (1.0 - sig_gate))).astype(
        jnp.bfloat16
    )
    up_grad = (hidden_grad * gate_out * sig_gate).astype(jnp.bfloat16)
    partial_value = lax.dot_general(
        gate_grad, gate_weight, (((1,), (1,)), ((), ())), preferred_element_type=jnp.float32
    )
    partial_value = partial_value + lax.dot_general(
        up_grad, up_weight, (((1,), (1,)), ((), ())), preferred_element_type=jnp.float32
    )
    norm_grad = scatter_axes(partial_value, TENSOR, (2, 0, 1), 1)
    offset = lax.axis_index(TENSOR) * col_count
    gain_cols = lax.dynamic_slice_in_dim(rms_gain, offset, col_count, 0)
    unit_cols = tokens.astype(jnp.float32) * inverse
    scaled = gain_cols * norm_grad
    row_sums = one_axis_at_a_time(jnp.sum(scaled * unit_cols, axis=-1), TENSOR)
    input_grad = output_grad.astype(jnp.float32) + inverse * (
        scaled - unit_cols * (row_sums / model_width)[:, None]
    )
    proj_grad = jnp.where(in_use[:, None], input_grad[positions], 0.0).astype(jnp.bfloat16)
    second_grad = lax.dot_general(
        proj_grad, act_full, (((0,), (0,)), ((), ())), preferred_element_type=jnp.float32
    )
    return (input_grad, second_grad)


def solution(mesh):
    torus = Mesh(
        mesh.devices.reshape(mesh.shape["groups"], 8, 8, 2),
        ("groups", "tensor_0", "tensor_1", "tensor_2"),
    )
    in_specs = (
        P("groups", TENSOR),
        P("groups"),
        P("groups"),
        P("groups"),
        P(),
        P(),
        P(TENSOR, None),
        P(TENSOR, None),
        P(TENSOR, None),
        P(),
        P(None, TENSOR),
        P(None, TENSOR),
        P(TENSOR, None),
        P("groups", TENSOR),
    )
    out_specs = (P("groups", TENSOR), P(GROUPS_TENSOR, None))
    return jax.shard_map(
        on_device, mesh=torus, in_specs=in_specs, out_specs=out_specs, check_vma=False
    )
```

profile of v0, /device:TPU:513, one launch (start us, length us, event | category | flops | bytes accessed | tf_op | source)
XLA Modules:
  0.0 529.5 jit_solution(11079233701716624059)
XLA Ops:
  14.7 21.0 %all-gather = bf16[640,100]{1,0:T(8,128)(2,1)S(1)} all-gather(bf16[80,100]{1,0:T(8,128)(2,1)S(1)} %gather_fusion.2), channel_id=2, replica_groups=mesh['groups'=2,'tensor_0'=8,'tensor_1'=8,'tensor_2'=2] {'tensor_0'}, dimensions={0}, use_global_device_ids=true | all-gather | bytes 144000 | tf_op jit(solution)/shard_map/all_gather | solution.py:21
  35.7 33.0 %all-gather.1 = bf16[64,80,100]{2,1,0:T(8,128)(2,1)} all-gather(bf16[8,80,100]{2,1,0:T(8,128)(2,1)S(1)} %bitcast.49), channel_id=3, replica_groups=mesh['groups'=2,'tensor_0'=8,'tensor_1'=8,'tensor_2'=2] {'tensor_1'}, dimensions={0}, use_global_device_ids=true | all-gather | bytes 1152000 | tf_op jit(solution)/shard_map/all_gather | solution.py:21
  70.8 11.6 %copy.40 = bf16[48,49152]{0,1:T(8,128)(2,1)} copy(bf16[48,49152]{1,0:T(8,128)(2,1)} %param.24) | data formatting | bytes 9437184 | tf_op args[8]
  82.5 6.9 %gather_fusion = bf16[256,48]{1,0:T(8,128)(2,1)S(1)} fusion(bf16[48,49152]{0,1:T(8,128)(2,1)} %copy.40, s32[1024]{0:T(1024)S(1)} %pad_clamp_fusion.2), kind=kCustom, calls=%fused_computation | custom fusion | bytes 50176 | tf_op jit(solution)/shard_map/jit(_take)/gather | solution.py:103
  89.5 17.5 %all-gather.11.cloned.1.call-done = bf16[16,8,80,100]{3,2,1,0:T(8,128)(2,1)} async-done(((bf16[8,8,80,100]{3,2,1,0:T(8,128)(2,1)}), bf16[16,8,80,100]{3,2,1,0:T(8,128)(2,1)}) %all-gather.11.cloned.1.call-update) | async-done | bytes 2048016 | tf_op jit(solution)/shard_map/all_gather | solution.py:21
  112.4 3.9 copy.43
  116.4 6.8 %reshape.107 = f32[80,12800]{1,0:T(8,128)} reshape(f32[80,128,100]{2,1,0:T(8,128)} %copy.43) | data formatting | bytes 8192000 | tf_op jit(solution)/shard_map/convert_element_type | solution.py:58
  125.7 3.5 fusion.4
  130.4 53.1 %all_gather.33 = bf16[80,6144]{0,1:T(8,128)(2,1)S(1)} all-gather(bf16[80,48]{0,1:T(8,128)(2,1)S(1)} %fusion.21), channel_id=1, replica_groups=mesh['groups'=2,'tensor_0'=8,'tensor_1'=8,'tensor_2'=2] {'tensor_0','ten..., dimensions={1}, use_global_device_ids=true | all-gather | bytes 990720 | tf_op jit(solution)/shard_map/all_gather | solution.py:98
  186.0 5.0 all-gather.9.cloned.1.call-done
  191.0 3.4 fusion.35
  194.4 77.7 %all-gather.7.cloned.1.call-done = bf16[256,6144]{0,1:T(8,128)(2,1)} async-done(((bf16[256,48]{0,1:T(8,128)(2,1)}), bf16[256,6144]{0,1:T(8,128)(2,1)}) %all-gather.7.cloned.1.call-update) | async-done | bytes 3145744 | tf_op jit(solution)/shard_map/all_gather | solution.py:105
  272.1 2.9 fusion
  275.0 3.5 fusion.10
  278.4 8.0 %fusion.9 = f32[256,6144]{1,0:T(8,128)} fusion(bf16[6144,128]{1,0:T(8,128)(2,1)} %param.26, f32[256,128]{1,0:T(8,128)S(1)} %fusion.35, bf16[6144,128]{1,0:T(8,128)(2,1)S(1)} %copy-done, bf16[256,6144]{0,1:T(8,128)(2,1)} %all-gather.7.cloned.1.call-done, f32[6144]{0:T(1024)S(1)} %copy-done.8, f32[256]{0:T(256)S(1)} %add_rsqrt_fusion, f32[256,128]{1,0:T(8,128)S(1)} %fusion.10), kind=kOutput, calls=%fused_computation.21 | convolution fusion | flops 811925504 | bytes 12870656 | tf_op jit(solution)/shard_map/dot_general | solution.py:122
  286.5 6.4 %convolution_add_fusion = f32[256,6144]{1,0:T(8,128)} fusion(f32[256,6144]{1,0:T(8,128)} %fusion.9, bf16[6144,128]{1,0:T(8,128)(2,1)S(1)} %copy-done, f32[256,128]{1,0:T(8,128)S(1)} %fusion.35, f32[256,128]{1,0:T(8,128)S(1)} %fusion.10), kind=kOutput, calls=%fused_computation.5 | convolution fusion | flops 404422656 | bytes 14417920 | tf_op jit(solution)/shard_map/dot_general | solution.py:125
  292.9 6.6 %copy.46 = f32[256,6144]{0,1:T(8,128)} copy(f32[256,6144]{1,0:T(8,128)} %convolution_add_fusion) | data formatting | bytes 12582912 | tf_op jit(solution)/shard_map/add | solution.py:125
  299.5 11.5 %copy.47 = f32[8,8,2,256,48]{4,3,1,0,2:T(8,128)} copy(f32[8,8,2,256,48]{3,4,2,1,0:T(8,128)} %bitcast.46) | data formatting | bytes 12582912 | tf_op jit(solution)/shard_map/reshape | solution.py:34
  311.2 30.2 %reduce-scatter.4.cloned.1.call-done = f32[64,256,48]{2,1,0:T(8,128)} async-done(((f32[128,256,48]{2,1,0:T(8,128)}), f32[64,256,48]{2,1,0:T(8,128)}) %reduce-scatter.4.cloned.1.call-update) | async-done | bytes 3145744 | tf_op jit(solution)/shard_map/reduce_scatter | solution.py:37
  341.5 98.7 %reduce-scatter.6.cloned.1.call-done = f32[8,256,48]{2,1,0:T(8,128)} async-done(((f32[64,256,48]{2,1,0:T(8,128)}), f32[8,256,48]{2,1,0:T(8,128)}) %reduce-scatter.6.cloned.1.call-update) | async-done | bytes 393232 | tf_op jit(solution)/shard_map/reduce_scatter | solution.py:37
  440.5 36.8 %reduce-scatter.8.cloned.1.call-done = f32[1,256,48]{2,1,0:T(8,128)} async-done(((f32[8,256,48]{2,1,0:T(8,128)}), f32[1,256,48]{2,1,0:T(8,128)}) %reduce-scatter.8.cloned.1.call-update) | async-done | bytes 49168 | tf_op jit(solution)/shard_map/reduce_scatter | solution.py:37
  478.3 13.2 %psum.21 = f32[256]{0:T(256)S(1)} all-reduce(f32[256]{0:T(256)S(1)} %multiply_reduce_fusion), channel_id=1, replica_groups=mesh['groups'=2,'tensor_0'=8,'tensor_1'=8,'tensor_2'=2] {'tensor_0'}, use_global_device_ids=true, to_apply=%region_9.10 | all-reduce | flops 256 | bytes 2048 | tf_op jit(solution)/shard_map/psum | solution.py:53
  491.5 12.4 %psum.22 = f32[256]{0:T(256)S(1)} all-reduce(f32[256]{0:T(256)S(1)} %psum.21), channel_id=1, replica_groups=mesh['groups'=2,'tensor_0'=8,'tensor_1'=8,'tensor_2'=2] {'tensor_1'}, use_global_device_ids=true, to_apply=%region_10.11 | all-reduce | flops 256 | bytes 2048 | tf_op jit(solution)/shard_map/psum | solution.py:53
  503.9 14.6 %psum.23 = f32[256]{0:T(256)S(1)} all-reduce(f32[256]{0:T(256)S(1)} %psum.22), channel_id=1, replica_groups=mesh['groups'=2,'tensor_0'=8,'tensor_1'=8,'tensor_2'=2] {'tensor_2'}, use_global_device_ids=true, to_apply=%region_11.12 | all-reduce | flops 256 | bytes 2048 | tf_op jit(solution)/shard_map/psum | solution.py:53
  (72 shorter events, 26.8 us)
Async XLA Ops:
  7.2 271.3 %copy-start = (bf16[6144,128]{1,0:T(8,128)(2,1)S(1)}, bf16[6144,128]{1,0:T(8,128)(2,1)}, u32[]{:S(2)}) copy-start(bf16[6144,128]{1,0:T(8,128)(2,1)} %param.27) | copy-start | bytes 4718596
  7.2 62.4 %copy-start.2 = (s32[128]{0:T(128)S(1)}, s32[128]{0:T(128)}, u32[]{:S(2)}) copy-start(s32[128]{0:T(128)} %param.18) | copy-start | bytes 1540
  7.2 99.8 %all-gather.11.cloned.1.call-start = ((), (), s32[]{:S(2)}) async-start(), calls=%async_computation.8 | async-start | bytes 3932160 | tf_op jit(solution)/shard_map/all_gather | solution.py:21
  68.7 122.3 %all-gather.9.cloned.1.call-start = ((), (), s32[]{:S(2)}) async-start(), calls=%async_computation.4 | async-start | bytes 3170304 | tf_op jit(solution)/shard_map/all_gather | solution.py:112
  69.5 202.6 %all-gather.7.cloned.1.call-start = ((), (), s32[]{:S(2)}) async-start(), calls=%async_computation.3 | async-start | bytes 3170304 | tf_op jit(solution)/shard_map/all_gather | solution.py:105
  70.8 11.6 %copy-start.9 = (s32[256]{0:T(256)S(1)}, s32[256]{0:T(256)}, u32[]{:S(2)}) copy-start(s32[256]{0:T(256)} %param.19) | copy-start | bytes 3076
  110.1 2.3 copy-start.3
  123.1 6.1 %copy-start.10 = (bf16[48,12800]{1,0:T(8,128)(2,1)S(1)}, bf16[48,12800]{1,0:T(8,128)(2,1)}, u32[]{:S(2)}) copy-start(bf16[48,12800]{1,0:T(8,128)(2,1)} %param.22) | copy-start | bytes 3686404
  125.7 3.7 copy-start.5
  125.7 3.7 copy-start.11
  125.7 3.7 copy-start.12
  129.4 54.1 %copy-start.6 = (bf16[48,6144]{1,0:T(8,128)(2,1)S(1)}, bf16[48,6144]{1,0:T(8,128)(2,1)}, u32[]{:S(2)}) copy-start(bf16[48,6144]{1,0:T(8,128)(2,1)} %param.23) | copy-start | bytes 1769476
  185.6 89.3 %copy-start.8 = (f32[6144]{0:T(1024)S(1)}, f32[6144]{0:T(1024)}, u32[]{:S(2)}) copy-start(f32[6144]{0:T(1024)} %param.25) | copy-start | bytes 73732
  185.7 155.7 %reduce-scatter.4.cloned.1.call-start = ((), (), s32[]{:S(2)}) async-start(), calls=%async_computation.5 | async-start | bytes 25165824 | tf_op jit(solution)/shard_map/reduce_scatter | solution.py:37
  272.1 2.9 copy-start.4
  311.1 129.1 %reduce-scatter.6.cloned.1.call-start = ((), (), s32[]{:S(2)}) async-start(), calls=%async_computation.6 | async-start | bytes 9437184 | tf_op jit(solution)/shard_map/reduce_scatter | solution.py:37
  341.3 98.9 %copy-start.7 = (bf16[256,48]{0,1:T(8,128)(2,1)S(1)}, bf16[256,48]{0,1:T(8,128)(2,1)}, u32[]{:S(2)}) copy-start(bf16[256,48]{0,1:T(8,128)(2,1)} %param.29) | copy-start | bytes 73732
  341.4 181.2 %copy-start.1 = (bf16[6144,128]{1,0:T(8,128)(2,1)S(1)}, bf16[6144,128]{1,0:T(8,128)(2,1)}, u32[]{:S(2)}) copy-start(bf16[6144,128]{1,0:T(8,128)(2,1)} %param.27) | copy-start | bytes 4718596
  341.4 135.8 %reduce-scatter.8.cloned.1.call-start = ((), (), s32[]{:S(2)}) async-start(), calls=%async_computation.7 | async-start | bytes 1179648 | tf_op jit(solution)/shard_map/reduce_scatter | solution.py:37
Sparse Core Ops, SparseCore 0:
  68.8 38.1 all-gather.10
  109.6 81.3 all-gather.8
  194.2 77.8 all-gather.6
  311.2 30.0 reduce-scatter.3
  343.7 96.3 reduce-scatter.5
  442.6 34.6 reduce-scatter.7
where the time goes:
time: 531 us; the launch traced here: 529 us
  waiting for transfers between devices  267 us (50%)
  blocking collectives  147 us (28%)
  local copies, waits for them, and re-layouts  57.9 us (11%)
  matrix products  24.4 us (5%)
  other arithmetic  18 us (3%)
  between operations  14.4 us (3%)
    reduce_scatter x3, waiting for transfers between devices, own_block(): parts = lax.psum_scatter(parts, axes[k], scatter_dimension=0, tiled=True)  166 us
    all_gather x1, waiting for transfers between devices, on_device(): full_tokens = lax.all_gather(tokens, TENSOR, axis=1, tiled=True)  77.7 us
    all_gather x2, blocking collectives, all_blocks(): parts = lax.all_gather(parts, axes[k])  54 us
    all_gather x1, blocking collectives, on_device(): act_full = lax.all_gather(act_cols, TENSOR, axis=1, tiled=True)  53.1 us
    psum x3, blocking collectives, one_axis_at_a_time(): x = lax.psum(x, axis)  40.2 us
    all_gather x1, waiting for transfers between devices, all_blocks(): parts = lax.all_gather(parts, axes[k])  17.5 us
    unnamed x30, local copies, waits for them, and re-layouts  15.8 us
    reshape x1, local copies, waits for them, and re-layouts, own_block(): parts = parts.reshape(*(lax.axis_size(a) for a in axes), *inside)  11.5 us
  transfers between devices with their start and end apart: 6, of which 6 were waited for; matrix products, arithmetic and copies ran while one was open for 9% of the time, Pallas kernels for 0%

commit v1 on v0

--- a/solution.py
+++ b/solution.py
@@ -95,7 +95,8 @@
         normed, proj_first, (((1,), (1,)), ((), ())), preferred_element_type=jnp.float32
     )
     act_cols = jax.nn.gelu(hidden_pre, approximate=False).astype(jnp.bfloat16)
-    act_full = lax.all_gather(act_cols, TENSOR, axis=1, tiled=True)
+    repeated = jnp.stack([act_cols] * lax.axis_size(TENSOR))
+    act_full = jnp.concatenate(lax.all_to_all(repeated, TENSOR, 0, 0), axis=1)
     projected = lax.dot_general(
         act_full, proj_second, (((1,), (1,)), ((), ())), preferred_element_type=jnp.float32
     ).astype(jnp.bfloat16)

time: 531 us -> 548 us (1.032)
  waiting for transfers between devices: 267 us -> 321 us
  blocking collectives: 147 us -> 93.8 us
  starting transfers between devices: 0.6 us -> 14.8 us
    all_gather x1 -> x0, blocking collectives: 53.1 us -> none  [on_device(): act_full = lax.all_gather(act_cols, TENSOR, axis=1, tiled=True)]
    all_to_all x0 -> x1, waiting for transfers between devices: none -> 21.1 us  [on_device(): act_full = jnp.concatenate(lax.all_to_all(repeated, TENSOR, 0, 0), axis=1)]
    all_gather x1, waiting for transfers between devices: 17.5 us -> 37.5 us  [all_blocks(): parts = lax.all_gather(parts, axes[k])]
    all_to_all x0 -> x1, starting transfers between devices: none -> 14.4 us  [on_device(): act_full = jnp.concatenate(lax.all_to_all(repeated, TENSOR, 0, 0), axis=1)]
    all_gather x1, waiting for transfers between devices: 5.05 us -> 17 us  [on_device(): lax.all_gather(output_grad, TENSOR, axis=1, tiled=True)]
    unnamed x30 -> x26, local copies, waits for them, and re-layouts: 15.8 us -> 15.8 us
  transfers between devices with their start and end apart: 6 -> 7, of which waited for: 6 -> 7; matrix products, arithmetic and copies ran while one was open for 9% -> 9% of each run, Pallas kernels for 0% -> 0%
where the time goes in v1:
time: 548 us; the launch traced here: 547 us
  waiting for transfers between devices  321 us (59%)
  blocking collectives  93.8 us (17%)
  local copies, waits for them, and re-layouts  59.3 us (11%)
  matrix products  25.6 us (5%)
  other arithmetic  18 us (3%)
  starting transfers between devices  14.8 us (3%)
  between operations  14.4 us (3%)
    reduce_scatter x3, waiting for transfers between devices, own_block(): parts = lax.psum_scatter(parts, axes[k], scatter_dimension=0, tiled=True)  166 us
    all_gather x1, waiting for transfers between devices, on_device(): full_tokens = lax.all_gather(tokens, TENSOR, axis=1, tiled=True)  78.4 us
    all_gather x2, blocking collectives, all_blocks(): parts = lax.all_gather(parts, axes[k])  54 us
    psum x3, blocking collectives, one_axis_at_a_time(): x = lax.psum(x, axis)  39.8 us
    all_gather x1, waiting for transfers between devices, all_blocks(): parts = lax.all_gather(parts, axes[k])  37.5 us
    all_to_all x1, waiting for transfers between devices, on_device(): act_full = jnp.concatenate(lax.all_to_all(repeated, TENSOR, 0, 0), axis=1)  21.1 us
    all_gather x1, waiting for transfers between devices, on_device(): lax.all_gather(output_grad, TENSOR, axis=1, tiled=True)  17 us
    unnamed x26, local copies, waits for them, and re-layouts  15.8 us
  transfers between devices with their start and end apart: 7, of which 7 were waited for; matrix products, arithmetic and copies ran while one was open for 9% of the time, Pallas kernels for 0%

profile of v1, /device:TPU:513, one launch (start us, length us, event | category | flops | bytes accessed | tf_op | source)
XLA Modules:
  0.0 546.8 jit_solution(17470224346475255569)
XLA Ops:
  14.6 21.0 %all-gather = bf16[640,100]{1,0:T(8,128)(2,1)S(1)} all-gather(bf16[80,100]{1,0:T(8,128)(2,1)S(1)} %gather_fusion.2), channel_id=2, replica_groups=mesh['groups'=2,'tensor_0'=8,'tensor_1'=8,'tensor_2'=2] {'tensor_0'}, dimensions={0}, use_global_device_ids=true | all-gather | bytes 144000 | tf_op jit(solution)/shard_map/all_gather | solution.py:21
  35.6 33.0 %all-gather.1 = bf16[64,80,100]{2,1,0:T(8,128)(2,1)} all-gather(bf16[8,80,100]{2,1,0:T(8,128)(2,1)S(1)} %bitcast.54), channel_id=3, replica_groups=mesh['groups'=2,'tensor_0'=8,'tensor_1'=8,'tensor_2'=2] {'tensor_1'}, dimensions={0}, use_global_device_ids=true | all-gather | bytes 1152000 | tf_op jit(solution)/shard_map/all_gather | solution.py:21
  69.5 37.5 %all-gather.11.cloned.1.call-done = bf16[16,8,80,100]{3,2,1,0:T(8,128)(2,1)} async-done(((bf16[8,8,80,100]{3,2,1,0:T(8,128)(2,1)}), bf16[16,8,80,100]{3,2,1,0:T(8,128)(2,1)}) %all-gather.11.cloned.1.call-update) | async-done | bytes 2048016 | tf_op jit(solution)/shard_map/all_gather | solution.py:21
  112.4 3.9 copy.44
  116.3 6.8 %reshape.117 = f32[80,12800]{1,0:T(8,128)} reshape(f32[80,128,100]{2,1,0:T(8,128)} %copy.44) | data formatting | bytes 8192000 | tf_op jit(solution)/shard_map/convert_element_type | solution.py:58
  125.7 3.5 fusion.4
  131.8 14.4 %all-to-all-start = ((bf16[128,80,48]{1,2,0:T(8,128)(2,1)}), bf16[128,80,48]{1,2,0:T(8,128)(2,1)S(1)}, u32[]{:S(2)}, u32[]{:S(2)}) async-start(bf16[128,80,48]{1,2,0:T(8,128)(2,1)} %stack.2), calls=%async_computation | async-start | bytes 3145728 | tf_op jit(solution)/shard_map/all_to_all | solution.py:99
  147.6 11.6 %copy.41 = bf16[48,49152]{0,1:T(8,128)(2,1)} copy(bf16[48,49152]{1,0:T(8,128)(2,1)} %param.24) | data formatting | bytes 9437184 | tf_op args[8]
  159.2 6.9 %gather_fusion = bf16[256,48]{1,0:T(8,128)(2,1)S(1)} fusion(bf16[48,49152]{0,1:T(8,128)(2,1)} %copy.41, s32[1024]{0:T(1024)S(1)} %pad_clamp_fusion.2), kind=kCustom, calls=%fused_computation | custom fusion | bytes 50176 | tf_op jit(solution)/shard_map/jit(_take)/gather | solution.py:104
  166.3 21.1 %all-to-all-done = bf16[128,80,48]{1,2,0:T(8,128)(2,1)S(1)} async-done(((bf16[128,80,48]{1,2,0:T(8,128)(2,1)}), bf16[128,80,48]{1,2,0:T(8,128)(2,1)S(1)}, u32[]{:S(2)}, u32[]{:S(2)}) %all-to-all-start) | async-done | bytes 983072 | tf_op jit(solution)/shard_map/all_to_all | solution.py:99
  190.6 17.0 %all-gather.9.cloned.1.call-done = bf16[256,6144]{0,1:T(8,128)(2,1)} async-done(((bf16[256,48]{0,1:T(8,128)(2,1)}), bf16[256,6144]{0,1:T(8,128)(2,1)}) %all-gather.9.cloned.1.call-update) | async-done | bytes 3145744 | tf_op jit(solution)/shard_map/all_gather | solution.py:113
  207.6 3.4 fusion.35
  211.0 78.4 %all-gather.7.cloned.1.call-done = bf16[256,6144]{0,1:T(8,128)(2,1)} async-done(((bf16[256,48]{0,1:T(8,128)(2,1)}), bf16[256,6144]{0,1:T(8,128)(2,1)}) %all-gather.7.cloned.1.call-update) | async-done | bytes 3145744 | tf_op jit(solution)/shard_map/all_gather | solution.py:106
  292.2 3.5 fusion.10
  295.7 8.0 %fusion.9 = f32[256,6144]{1,0:T(8,128)} fusion(bf16[6144,128]{1,0:T(8,128)(2,1)} %param.26, f32[256,128]{1,0:T(8,128)S(1)} %fusion.35, bf16[6144,128]{1,0:T(8,128)(2,1)S(1)} %copy-done, bf16[256,6144]{0,1:T(8,128)(2,1)} %all-gather.7.cloned.1.call-done, f32[6144]{0:T(1024)S(1)} %copy-done.6, f32[256]{0:T(256)S(1)} %add_rsqrt_fusion, f32[256,128]{1,0:T(8,128)S(1)} %fusion.10), kind=kOutput, calls=%fused_computation.21 | convolution fusion | flops 811925504 | bytes 12870656 | tf_op jit(solution)/shard_map/dot_general | solution.py:123
  303.8 6.4 %convolution_add_fusion = f32[256,6144]{1,0:T(8,128)} fusion(f32[256,6144]{1,0:T(8,128)} %fusion.9, bf16[6144,128]{1,0:T(8,128)(2,1)S(1)} %copy-done, f32[256,128]{1,0:T(8,128)S(1)} %fusion.35, f32[256,128]{1,0:T(8,128)S(1)} %fusion.10), kind=kOutput, calls=%fused_computation.5 | convolution fusion | flops 404422656 | bytes 14417920 | tf_op jit(solution)/shard_map/dot_general | solution.py:126
  310.2 6.6 %copy.47 = f32[256,6144]{0,1:T(8,128)} copy(f32[256,6144]{1,0:T(8,128)} %convolution_add_fusion) | data formatting | bytes 12582912 | tf_op jit(solution)/shard_map/add | solution.py:126
  316.8 11.5 %copy.48 = f32[8,8,2,256,48]{4,3,1,0,2:T(8,128)} copy(f32[8,8,2,256,48]{3,4,2,1,0:T(8,128)} %bitcast.49) | data formatting | bytes 12582912 | tf_op jit(solution)/shard_map/reshape | solution.py:34
  328.5 30.1 %reduce-scatter.4.cloned.1.call-done = f32[64,256,48]{2,1,0:T(8,128)} async-done(((f32[128,256,48]{2,1,0:T(8,128)}), f32[64,256,48]{2,1,0:T(8,128)}) %reduce-scatter.4.cloned.1.call-update) | async-done | bytes 3145744 | tf_op jit(solution)/shard_map/reduce_scatter | solution.py:37
  358.8 98.7 %reduce-scatter.6.cloned.1.call-done = f32[8,256,48]{2,1,0:T(8,128)} async-done(((f32[64,256,48]{2,1,0:T(8,128)}), f32[8,256,48]{2,1,0:T(8,128)}) %reduce-scatter.6.cloned.1.call-update) | async-done | bytes 393232 | tf_op jit(solution)/shard_map/reduce_scatter | solution.py:37
  457.7 37.2 %reduce-scatter.8.cloned.1.call-done = f32[1,256,48]{2,1,0:T(8,128)} async-done(((f32[8,256,48]{2,1,0:T(8,128)}), f32[1,256,48]{2,1,0:T(8,128)}) %reduce-scatter.8.cloned.1.call-update) | async-done | bytes 49168 | tf_op jit(solution)/shard_map/reduce_scatter | solution.py:37
  496.1 12.7 %psum.21 = f32[256]{0:T(256)S(1)} all-reduce(f32[256]{0:T(256)S(1)} %multiply_reduce_fusion), channel_id=1, replica_groups=mesh['groups'=2,'tensor_0'=8,'tensor_1'=8,'tensor_2'=2] {'tensor_0'}, use_global_device_ids=true, to_apply=%region_9.10 | all-reduce | flops 256 | bytes 2048 | tf_op jit(solution)/shard_map/psum | solution.py:53
  508.8 12.4 %psum.22 = f32[256]{0:T(256)S(1)} all-reduce(f32[256]{0:T(256)S(1)} %psum.21), channel_id=1, replica_groups=mesh['groups'=2,'tensor_0'=8,'tensor_1'=8,'tensor_2'=2] {'tensor_1'}, use_global_device_ids=true, to_apply=%region_10.11 | all-reduce | flops 256 | bytes 2048 | tf_op jit(solution)/shard_map/psum | solution.py:53
  521.1 14.7 %psum.23 = f32[256]{0:T(256)S(1)} all-reduce(f32[256]{0:T(256)S(1)} %psum.22), channel_id=1, replica_groups=mesh['groups'=2,'tensor_0'=8,'tensor_1'=8,'tensor_2'=2] {'tensor_2'}, use_global_device_ids=true, to_apply=%region_11.12 | all-reduce | flops 256 | bytes 2048 | tf_op jit(solution)/shard_map/psum | solution.py:53
  (70 shorter events, 32.0 us)
Async XLA Ops:
  7.2 288.6 %copy-start = (bf16[6144,128]{1,0:T(8,128)(2,1)S(1)}, bf16[6144,128]{1,0:T(8,128)(2,1)}, u32[]{:S(2)}) copy-start(bf16[6144,128]{1,0:T(8,128)(2,1)} %param.27) | copy-start | bytes 4718596
  7.2 99.8 %all-gather.11.cloned.1.call-start = ((), (), s32[]{:S(2)}) async-start(), calls=%async_computation.9 | async-start | bytes 3932160 | tf_op jit(solution)/shard_map/all_gather | solution.py:21
  68.7 138.9 %all-gather.9.cloned.1.call-start = ((), (), s32[]{:S(2)}) async-start(), calls=%async_computation.5 | async-start | bytes 3170304 | tf_op jit(solution)/shard_map/all_gather | solution.py:113
  110.1 2.3 copy-start.2
  123.1 6.1 %copy-start.8 = (bf16[48,12800]{1,0:T(8,128)(2,1)S(1)}, bf16[48,12800]{1,0:T(8,128)(2,1)}, u32[]{:S(2)}) copy-start(bf16[48,12800]{1,0:T(8,128)(2,1)} %param.22) | copy-start | bytes 3686404
  125.6 3.7 copy-start.4
  125.7 3.7 copy-start.9
  125.7 3.7 copy-start.10
  130.4 15.9 %copy-start.1 = (s32[128]{0:T(128)S(1)}, s32[128]{0:T(128)}, u32[]{:S(2)}) copy-start(s32[128]{0:T(128)} %param.18) | copy-start | bytes 1540
  131.8 55.5 %all-to-all-start = ((bf16[128,80,48]{1,2,0:T(8,128)(2,1)}), bf16[128,80,48]{1,2,0:T(8,128)(2,1)S(1)}, u32[]{:S(2)}, u32[]{:S(2)}) async-start(bf16[128,80,48]{1,2,0:T(8,128)(2,1)} %stack.2), calls=%async_computation | async-start | bytes 3145728 | tf_op jit(solution)/shard_map/all_to_all | solution.py:99
  146.2 143.1 %all-gather.7.cloned.1.call-start = ((), (), s32[]{:S(2)}) async-start(), calls=%async_computation.4 | async-start | bytes 3170304 | tf_op jit(solution)/shard_map/all_gather | solution.py:106
  147.6 11.6 %copy-start.7 = (s32[256]{0:T(256)S(1)}, s32[256]{0:T(256)}, u32[]{:S(2)}) copy-start(s32[256]{0:T(256)} %param.19) | copy-start | bytes 3076
  190.6 101.7 %copy-start.6 = (f32[6144]{0:T(1024)S(1)}, f32[6144]{0:T(1024)}, u32[]{:S(2)}) copy-start(f32[6144]{0:T(1024)} %param.25) | copy-start | bytes 73732
  190.6 168.1 %reduce-scatter.4.cloned.1.call-start = ((), (), s32[]{:S(2)}) async-start(), calls=%async_computation.6 | async-start | bytes 25165824 | tf_op jit(solution)/shard_map/reduce_scatter | solution.py:37
  289.3 2.9 copy-start.3
  328.4 129.0 %reduce-scatter.6.cloned.1.call-start = ((), (), s32[]{:S(2)}) async-start(), calls=%async_computation.7 | async-start | bytes 9437184 | tf_op jit(solution)/shard_map/reduce_scatter | solution.py:37
  358.6 98.9 %copy-start.5 = (bf16[256,48]{0,1:T(8,128)(2,1)S(1)}, bf16[256,48]{0,1:T(8,128)(2,1)}, u32[]{:S(2)}) copy-start(bf16[256,48]{0,1:T(8,128)(2,1)} %param.29) | copy-start | bytes 73732
  358.7 136.3 %reduce-scatter.8.cloned.1.call-start = ((), (), s32[]{:S(2)}) async-start(), calls=%async_computation.8 | async-start | bytes 1179648 | tf_op jit(solution)/shard_map/reduce_scatter | solution.py:37
Sparse Core Ops, SparseCore 0:
  68.8 38.1 all-gather.10
  109.6 97.9 all-gather.8
  210.8 78.5 all-gather.6
  328.5 30.0 reduce-scatter.3
  361.0 96.3 reduce-scatter.5
  459.9 35.0 reduce-scatter.7
